TPU v7x, 256 devices: a whole 4x4x8 slice. The times are simulated.
256 devices in a mesh: ta: 8 (over x, z_lo), sa: 32 (over z_hi, y, core).
Axes of the slice: x: 4, y: 4, z: 8 (z_hi: 4, z_lo: 2; z = z_hi * 2 + z_lo), core: 2. Of those that a mesh axis runs over, the one named last changes fastest.
Arguments:
- eigvecs: bfloat16 [48, 2, 3, 13824, 128], P('ta', None, None, 'sa'), may hold values from -0.0390625 to 0.0390625
- solutions: bfloat16 [48, 2, 3, 13824, 128], P('ta', None, None, 'sa'), may hold values from -6 to 6
Outputs:
- tau: float32 [48, 2, 128, 128], P('ta', None, 'sa')
- corr: float32 [48], replicated
All inputs are finite; a program needn't handle non-finite values.
Results may differ from a plain program's by a relative error of at most 0.0003.
Values sent between devices are 32-bit elements; how exact they have to be, the bound alone decides.
A program may use at most 64 MiB of HBM per device.

v0:
```python
import jax
import jax.numpy as jnp
from jax import lax
from jax.sharding import PartitionSpec as P


def split_up(array, dim, length):
    before, after = (array.shape[:dim], array.shape[dim + 1 :])
    return jnp.moveaxis(array.reshape(*before, length, -1, *after), dim, 0)


def sum_at_owner(array, axis, dim):
    length = lax.axis_size(axis)
    tiles = lax.all_to_all(split_up(array, dim, length), axis, 0, 0, tiled=True)
    return jnp.sum(tiles, axis=0)


def from_everyone(array, axis):
    copies = jnp.broadcast_to(array, (lax.axis_size(axis), *array.shape))
    return lax.all_to_all(copies, axis, split_axis=0, concat_axis=0, tiled=True)


def taken_together(array, axis):
    return from_everyone(array, axis).sum(axis=0)


def in_order(tiles, dim):
    tiles = jnp.moveaxis(tiles, 0, dim)
    lengths = tiles.shape
    return tiles.reshape(*lengths[:dim], lengths[dim] * lengths[dim + 1], *lengths[dim + 2 :])


def gather_directly(array, axis, dim):
    return in_order(from_everyone(array, axis), dim)


def per_device(eigvecs, solutions):
    slices = eigvecs.shape[0]
    vec_re = eigvecs[:, 0].reshape(slices, -1, eigvecs.shape[-1])
    vec_im = eigvecs[:, 1].reshape(slices, -1, eigvecs.shape[-1])
    sol_re = solutions[:, 0].reshape(slices, -1, solutions.shape[-1])
    sol_im = solutions[:, 1].reshape(slices, -1, solutions.shape[-1])

    def contract(left, right):
        return jnp.einsum("tka,tkb->tab", left, right, preferred_element_type=jnp.float32)

    real_part = contract(vec_re, sol_re) + contract(vec_im, sol_im)
    imag_part = contract(vec_re, sol_im) - contract(vec_im, sol_re)
    partial_tau = jnp.stack([real_part, imag_part], 1)
    scale = 1.0 / (2.0 * partial_tau.shape[2] * partial_tau.shape[3])
    tau = sum_at_owner(partial_tau, "sa", 2)
    row_norms = jnp.sum(tau * tau, axis=(1, 2, 3))
    corr_local = taken_together(row_norms, "sa") * scale
    corr = gather_directly(corr_local, "ta", 0)
    return (tau, corr)


def solution(mesh):
    in_specs = (P("ta", None, None, "sa", None), P("ta", None, None, "sa", None))
    out_specs = (P("ta", None, "sa", None), P())
    return jax.shard_map(
        per_device, mesh=mesh, in_specs=in_specs, out_specs=out_specs, check_vma=False
    )
```

profile of v0, /device:TPU:1, one launch (start us, length us, event | category | flops | bytes accessed | tf_op | source)
XLA Modules:
  0.0 69.8 jit_solution(4066686653678591434)
XLA Ops:
  0.6 0.0 copy-start
  0.6 2.6 %fusion.1 = (bf16[6,1,3,432,128]{4,3,2,1,0:T(8,128)(2,1)S(1)}, bf16[6,1,3,432,128]{4,3,2,1,0:T(8,128)(2,1)S(1)}) fusion(bf16[6,2,3,432,128]{4,3,2,1,0:T(8,128)(2,1)} %param.2), kind=kLoop, calls=%fused_computation.7 | loop fusion | bytes 7962624 | tf_op jit(solution)/shard_map/slice | solution.py:40
  3.2 0.7 %copy-done = bf16[6,2,3,432,128]{4,3,2,1,0:T(8,128)(2,1)S(1)} copy-done((bf16[6,2,3,432,128]{4,3,2,1,0:T(8,128)(2,1)S(1)}, bf16[6,2,3,432,128]{4,3,2,1,0:T(8,128)(2,1)}, u32[]{:S(2)}) %copy-start) | copy-done | bytes 3981336
  4.0 0.3 fusion
  4.2 0.9 %fusion.2 = f32[6,128,128]{2,1,0:T(8,128)S(1)} fusion(bf16[6,1296,128]{2,1,0:T(8,128)(2,1)S(1)} %bitcast.20, bf16[6,1296,128]{2,1,0:T(8,128)(2,1)S(1)} %bitcast.18), kind=kOutput, calls=%fused_computation.8 | convolution fusion | flops 254803968 | bytes 4374528 | tf_op jit(solution)/shard_map/tka,tkb->tab/dot_general | solution.py:45
  5.1 0.9 %fusion.3 = f32[6,128,128]{2,1,0:T(8,128)S(1)} fusion(bf16[6,1296,128]{2,1,0:T(8,128)(2,1)S(1)} %bitcast.21, bf16[6,1296,128]{2,1,0:T(8,128)(2,1)S(1)} %bitcast.22), kind=kOutput, calls=%fused_computation.9 | convolution fusion | flops 254803968 | bytes 4374528 | tf_op jit(solution)/shard_map/tka,tkb->tab/dot_general | solution.py:45
  5.9 0.9 %convolution_add_fusion = f32[6,128,128]{2,1,0:T(8,128)S(1)} fusion(f32[6,128,128]{2,1,0:T(8,128)S(1)} %fusion.2, bf16[6,1296,128]{2,1,0:T(8,128)(2,1)S(1)} %bitcast.16, bf16[6,1296,128]{2,1,0:T(8,128)(2,1)S(1)} %bitcast.23), kind=kOutput, calls=%fused_computation.1 | convolution fusion | flops 254902272 | bytes 4767744 | tf_op jit(solution)/shard_map/tka,tkb->tab/dot_general | solution.py:45
  6.8 0.9 %convolution_subtract_fusion = f32[6,128,128]{2,1,0:T(8,128)S(1)} fusion(f32[6,128,128]{2,1,0:T(8,128)S(1)} %fusion.3, bf16[6,1296,128]{2,1,0:T(8,128)(2,1)S(1)} %bitcast.17, bf16[6,1296,128]{2,1,0:T(8,128)(2,1)S(1)} %bitcast.19), kind=kOutput, calls=%fused_computation | convolution fusion | flops 254902272 | bytes 4767744 | tf_op jit(solution)/shard_map/tka,tkb->tab/dot_general | solution.py:45
  7.7 0.2 copy_bitcast_fusion
  7.9 34.9 %all_to_all.17 = f32[32,6,2,4,128]{4,3,1,2,0:T(4,128)S(1)} all-to-all(f32[32,6,2,4,128]{4,3,1,2,0:T(4,128)S(1)} %copy_bitcast_fusion), channel_id=1, replica_groups=mesh['ta'=8,'sa'=32] {'sa'}, dimensions={0} | all-to-all | bytes 1572864 | tf_op jit(solution)/shard_map/all_to_all | solution.py:14
  42.7 0.1 reduce_sum.27
  42.9 0.1 multiply_reduce_fusion
  43.0 15.3 %all_to_all.18 = f32[32,1,6]{2,1,0:T(1,128)S(1)} all-to-all(f32[32,1,6]{2,1,0:T(1,128)S(1)} %broadcast_in_dim.6), channel_id=1, replica_groups=mesh['ta'=8,'sa'=32] {'sa'}, dimensions={0} | all-to-all | bytes 1536 | tf_op jit(solution)/shard_map/all_to_all | solution.py:20
  58.3 0.1 reduce_sum.29
  58.4 0.6 broadcast_in_dim.7
  59.0 4.0 %all-to-all-start.2 = ((f32[8,1,6]{2,1,0:T(1,128)}), f32[8,1,6]{2,1,0:T(1,128)S(1)}, u32[]{:S(2)}, u32[]{:S(2)}) async-start(f32[8,1,6]{2,1,0:T(1,128)} %broadcast_in_dim.7), calls=%async_computation.2 | async-start | bytes 8192 | tf_op jit(solution)/shard_map/all_to_all | solution.py:20
  63.0 0.6 copy.21
  63.6 4.4 %all-to-all-done.2 = f32[8,1,6]{2,1,0:T(1,128)S(1)} async-done(((f32[8,1,6]{2,1,0:T(1,128)}), f32[8,1,6]{2,1,0:T(1,128)S(1)}, u32[]{:S(2)}, u32[]{:S(2)}) %all-to-all-start.2) | async-done | bytes 224 | tf_op jit(solution)/shard_map/all_to_all | solution.py:20
  68.0 0.5 broadcast.14
  68.6 0.7 reduce.4
  69.2 0.6 reshape.21
  (2 shorter events, 0.0 us)
Async XLA Ops:
  0.6 3.3 %copy-start = (bf16[6,2,3,432,128]{4,3,2,1,0:T(8,128)(2,1)S(1)}, bf16[6,2,3,432,128]{4,3,2,1,0:T(8,128)(2,1)}, u32[]{:S(2)}) copy-start(bf16[6,2,3,432,128]{4,3,2,1,0:T(8,128)(2,1)} %param.3) | copy-start | bytes 11943940
  59.0 9.1 %all-to-all-start.2 = ((f32[8,1,6]{2,1,0:T(1,128)}), f32[8,1,6]{2,1,0:T(1,128)S(1)}, u32[]{:S(2)}, u32[]{:S(2)}) async-start(f32[8,1,6]{2,1,0:T(1,128)} %broadcast_in_dim.7), calls=%async_computation.2 | async-start | bytes 8192 | tf_op jit(solution)/shard_map/all_to_all | solution.py:20
where the time goes:
time: 70 us; the launch traced here: 69.8 us
  blocking collectives  50.2 us (72%)
  local copies, waits for them, and re-layouts  5.9 us (8%)
  waiting for transfers between devices  4.41 us (6%)
  starting transfers between devices  4.03 us (6%)
  matrix products  3.44 us (5%)
  other arithmetic  1.15 us (2%)
    all_to_all x1, blocking collectives, sum_at_owner(): tiles = lax.all_to_all(split_up(array, dim, length), axis, 0, 0, tiled=True)  34.9 us
    all_to_all x1, blocking collectives, from_everyone(): return lax.all_to_all(copies, axis, split_axis=0, concat_axis=0, tiled=True)  15.3 us
    all_to_all x1, waiting for transfers between devices, from_everyone(): return lax.all_to_all(copies, axis, split_axis=0, concat_axis=0, tiled=True)  4.41 us
    all_to_all x1, starting transfers between devices, from_everyone(): return lax.all_to_all(copies, axis, split_axis=0, concat_axis=0, tiled=True)  4.03 us
    dot_general x4, matrix products, contract(): jnp.einsum('tka,tkb->tab', left, right, preferred_element_type=jnp.float32)  3.44 us
    slice x1, local copies, waits for them, and re-layouts, per_device(): vec_im = eigvecs[:, 1].reshape(slices, -1, eigvecs.shape[-1])  2.57 us
  transfers between devices with their start and end apart: 1, of which 1 were waited for; matrix products, arithmetic and copies ran while one was open for 1% of the time, Pallas kernels for 0%

commit v1 on v0

v1 whole, which is shorter than its diff:
```python
import functools

import jax
import jax.numpy as jnp
from jax import lax
from jax.experimental import pallas as pl
from jax.experimental.pallas import tpu as pltpu
from jax.sharding import PartitionSpec as P

MESH = pl.DeviceIdType.MESH
X, Y, ZH, ZL, CORES = 4, 4, 4, 2, 2
Z = ZH * ZL
NT = 6
TG = 1
NG = NT // TG
BARRIER_AFTER = 3
F32 = jnp.float32


def position():
    ta, sa = lax.axis_index("ta"), lax.axis_index("sa")
    x, zl = lax.div(ta, ZL), lax.rem(ta, ZL)
    zh, y, core = lax.div(sa, Y * CORES), lax.rem(lax.div(sa, CORES), Y), lax.rem(sa, CORES)
    return x, y, zh, zl, core


def device(x, y, zh, zl, core):
    return (x * ZL + zl, (zh * Y + y) * CORES + core)


def kernel(
    scale, v_hbm, p_hbm, tau_ref, corr_ref,
    vbuf, pbuf, csend, keep, crecv, ysend, yrecv, zsend, zrecv, row1, recv1, row2, recv2,
    in_sem, csem_s, csem_r, ysem_s, ysem_r, zsem_s, zsem_r, nsem,
):
    x, y, zh, zl, core = position()
    z = zh * ZL + zl

    def load(t):
        return [
            pltpu.make_async_copy(v_hbm.at[t], vbuf.at[t], in_sem.at[t, 0]),
            pltpu.make_async_copy(p_hbm.at[t], pbuf.at[t], in_sem.at[t, 1]),
        ]

    peers1, peers2 = [], []
    for dz in range(Z):
        for dc in range(CORES):
            if dz or dc:
                zz = lax.rem(z + dz, Z)
                peers1.append((dz * CORES + dc, device(x, y, lax.div(zz, ZL), lax.rem(zz, ZL), lax.rem(core + dc, CORES))))
    for dx in range(X):
        for dy in range(Y):
            if dx or dy:
                peers2.append((dx * Y + dy, device(lax.rem(x + dx, X), lax.rem(y + dy, Y), zh, zl, core)))

    for copy in load(0):
        copy.start()
    barrier = pltpu.get_barrier_semaphore()
    for _, peer in peers1 + peers2:
        pl.semaphore_signal(barrier, inc=1, device_id=peer, device_id_type=MESH)
    for t in range(1, NT):
        for copy in load(t):
            copy.start()

    def remote(src, dst, send, recv, peer):
        return pltpu.make_async_remote_copy(
            src_ref=src, dst_ref=dst, send_sem=send, recv_sem=recv, device_id=peer, device_id_type=MESH
        )

    def to_core(t):
        return remote(csend.at[t], crecv.at[t], csem_s.at[t], csem_r.at[t], device(x, y, zh, zl, 1 - core))

    low = lax.broadcasted_iota(jnp.int32, (128, 128), 0) % 8 < 4
    first = core == 0
    for t in range(NT):
        for copy in load(t):
            copy.wait()
        v = jnp.concatenate([vbuf[t, 0], vbuf[t, 1]], axis=1)
        p = jnp.concatenate([pbuf[t, 0], pbuf[t, 1]], axis=1)
        o = lax.dot_general(v, p, (((0,), (0,)), ((), ())), preferred_element_type=F32)
        re = o[:128, :128] + o[128:, 128:]
        im = o[:128, 128:] - o[128:, :128]
        for0 = jnp.where(low, re, pltpu.roll(im, 4, 0))
        for1 = jnp.where(low, pltpu.roll(re, 124, 0), im)
        mine = jnp.where(first, for0, for1)
        other = jnp.where(first, for1, for0)
        csend[t] = other.reshape(ZH * Y, 8, 128)
        keep[t] = mine.reshape(ZH * Y, 8, 128)
        if t == BARRIER_AFTER:
            pl.semaphore_wait(barrier, len(peers1) + len(peers2))
            for s in range(t + 1):
                to_core(s).start()
        elif t > BARRIER_AFTER:
            to_core(t).start()

    def to_y(g, d):
        yy = lax.rem(y + d, Y)
        return remote(
            ysend.at[g, yy], yrecv.at[g, d - 1], ysem_s.at[g, d - 1], ysem_r.at[g, d - 1], device(x, yy, zh, zl, core)
        )

    def to_z(g, d):
        zz = lax.rem(zh + d, ZH)
        return remote(
            zsend.at[g, zz], zrecv.at[g, d - 1], zsem_s.at[g, d - 1], zsem_r.at[g, d - 1], device(x, y, zz, zl, core)
        )

    for g in range(NG):
        for i in range(TG):
            t = g * TG + i
            to_core(t).wait_recv()
            total = (keep[t] + crecv[t]).reshape(ZH, Y, 8, 128)
            for yy in range(Y):
                ysend[g, yy, i] = total[:, yy]
        for d in (2, 1, 3):
            to_y(g, d).start()
    for g in range(NG):
        for d in (1, 3, 2):
            to_y(g, d).wait_recv()
        total = ysend[g, y] + yrecv[g, 0] + yrecv[g, 1] + yrecv[g, 2]
        for zz in range(ZH):
            zsend[g, zz] = total[:, zz]
        for d in (2, 1, 3):
            to_z(g, d).start()
    lane = lax.broadcasted_iota(jnp.int32, (1, 128), 1)
    slot = (x * ZL + zl) * NT
    row = jnp.zeros((1, 128), F32)
    for g in range(NG):
        for d in (1, 3, 2):
            to_z(g, d).wait_recv()
        total = zsend[g, zh] + zrecv[g, 0] + zrecv[g, 1] + zrecv[g, 2]
        for i in range(TG):
            t = g * TG + i
            tau_ref[t] = total[i]
            norm = jnp.sum(total[i] * total[i], axis=(0, 1), keepdims=True)
            row = row + jnp.where(lane == slot + t, norm, 0.0)

    def share(row, own, recv, peers, stage):
        own[...] = row
        recv[0:1] = row
        for k, peer in peers:
            remote(own, recv.at[pl.ds(k, 1)], nsem.at[stage, 0], nsem.at[stage, 1], peer).start()
        rest = pltpu.make_async_copy(recv.at[pl.ds(1, len(peers))], recv.at[pl.ds(1, len(peers))], nsem.at[stage, 1])
        rest.wait()
        return jnp.sum(recv[...], axis=0, keepdims=True)

    row = share(row, row1, recv1, peers1, 0)
    row = share(row, row2, recv2, peers2, 1)
    corr_ref[...] = row * scale

    for stage, recv, peers in ((0, recv1, peers1), (1, recv2, peers2)):
        pltpu.make_async_copy(recv.at[pl.ds(1, len(peers))], recv.at[pl.ds(1, len(peers))], nsem.at[stage, 0]).wait()
    for t in range(NT):
        to_core(t).wait_send()
    for g in range(NG):
        for d in range(1, Y):
            to_y(g, d).wait_send()
        for d in range(1, ZH):
            to_z(g, d).wait_send()


def per_device(eigvecs, solutions):
    rows = eigvecs.shape[2] * eigvecs.shape[3]
    v = eigvecs.reshape(NT, 2, rows, 128)
    p = solutions.reshape(NT, 2, rows, 128)
    vmem = pl.BlockSpec(memory_space=pltpu.VMEM)
    hbm = pl.BlockSpec(memory_space=pltpu.HBM)
    tau, corr = pl.pallas_call(
        functools.partial(kernel, 1.0 / (2.0 * 128 * 128)),
        out_shape=(jax.ShapeDtypeStruct((NT, 8, 128), F32), jax.ShapeDtypeStruct((1, 128), F32)),
        in_specs=[hbm, hbm],
        out_specs=(vmem, vmem),
        scratch_shapes=[
            pltpu.VMEM((NT, 2, rows, 128), jnp.bfloat16),
            pltpu.VMEM((NT, 2, rows, 128), jnp.bfloat16),
            pltpu.VMEM((NT, ZH * Y, 8, 128), F32),
            pltpu.VMEM((NT, ZH * Y, 8, 128), F32),
            pltpu.VMEM((NT, ZH * Y, 8, 128), F32),
            pltpu.VMEM((NG, Y, TG, ZH, 8, 128), F32),
            pltpu.VMEM((NG, Y - 1, TG, ZH, 8, 128), F32),
            pltpu.VMEM((NG, ZH, TG, 8, 128), F32),
            pltpu.VMEM((NG, ZH - 1, TG, 8, 128), F32),
            pltpu.VMEM((1, 128), F32),
            pltpu.VMEM((Z * CORES, 128), F32),
            pltpu.VMEM((1, 128), F32),
            pltpu.VMEM((X * Y, 128), F32),
            pltpu.SemaphoreType.DMA((NT, 2)),
            pltpu.SemaphoreType.DMA((NT,)),
            pltpu.SemaphoreType.DMA((NT,)),
            pltpu.SemaphoreType.DMA((NG, Y - 1)),
            pltpu.SemaphoreType.DMA((NG, Y - 1)),
            pltpu.SemaphoreType.DMA((NG, ZH - 1)),
            pltpu.SemaphoreType.DMA((NG, ZH - 1)),
            pltpu.SemaphoreType.DMA((2, 2)),
        ],
        compiler_params=pltpu.CompilerParams(collective_id=0, has_side_effects=True, vmem_limit_bytes=60 * 1024 * 1024),
    )(v, p)
    return tau.reshape(NT, 2, 4, 128), corr[0, :48]


def solution(mesh):
    in_specs = (P("ta", None, None, "sa", None), P("ta", None, None, "sa", None))
    out_specs = (P("ta", None, "sa", None), P())
    return jax.shard_map(
        per_device, mesh=mesh, in_specs=in_specs, out_specs=out_specs, check_vma=False
    )
```

time: 70 us -> 36.5 us (0.52)
  blocking collectives: 50.2 us -> 0 us
  Pallas kernels: 0 us -> 33.2 us
  waiting for transfers between devices: 4.41 us -> 0 us
  starting transfers between devices: 4.03 us -> 0 us
  matrix products: 3.44 us -> 0 us
  local copies, waits for them, and re-layouts: 5.9 us -> 2.52 us
  other arithmetic: 1.15 us -> 0 us
    all_to_all x2 -> x0, blocking collectives: 50.2 us -> none  [the longest x1 34.9 us: sum_at_owner(): tiles = lax.all_to_all(split_up(array, dim, length), axis, 0, 0, tiled=True)]
    pallas_call x0 -> x1, Pallas kernels: none -> 33.2 us  [per_device(): pl.pallas_call(functools.partial(kernel, 1.0 / (2.0 * 128 * 128)), out_sh...]
    all_to_all x1 -> x0, waiting for transfers between devices: 4.41 us -> none  [from_everyone(): return lax.all_to_all(copies, axis, split_axis=0, concat_axis=0, tiled=True)]
    all_to_all x1 -> x0, starting transfers between devices: 4.03 us -> none  [from_everyone(): return lax.all_to_all(copies, axis, split_axis=0, concat_axis=0, tiled=True)]
    dot_general x4 -> x0, matrix products: 3.44 us -> none  [contract(): jnp.einsum('tka,tkb->tab', left, right, preferred_element_type=jnp.float32)]
    slice x2 -> x0, local copies, waits for them, and re-layouts: 2.82 us -> none  [the longest x1 2.57 us: per_device(): vec_im = eigvecs[:, 1].reshape(slices, -1, eigvecs.shape[-1])]
    squeeze x0 -> x1, local copies, waits for them, and re-layouts: none -> 1.18 us  [per_device(): return (tau.reshape(NT, 2, 4, 128), corr[0, :48])]
  transfers between devices with their start and end apart: 1 -> 0, of which waited for: 1 -> 0; matrix products, arithmetic and copies ran while one was open for 1% -> 0% of each run, Pallas kernels for 0% -> 0%
where the time goes in v1:
time: 36.5 us; the launch traced here: 36.3 us
  Pallas kernels  33.2 us (91%)
  local copies, waits for them, and re-layouts  2.52 us (7%)
  between operations  0.64 us (2%)
    pallas_call x1, Pallas kernels, per_device(): pl.pallas_call(functools.partial(kernel, 1.0 / (2.0 * 128 * 128)), out_sh...  33.2 us
    unnamed x1, local copies, waits for them, and re-layouts  1.35 us
    squeeze x1, local copies, waits for them, and re-layouts, per_device(): return (tau.reshape(NT, 2, 4, 128), corr[0, :48])  1.18 us

profile of v1, /device:TPU:1, one launch (start us, length us, event | category | flops | bytes accessed | tf_op | source)
XLA Modules:
  0.0 36.3 jit_solution(1188125726740979975)
XLA Ops:
  0.6 33.2 %shard_map.41 = (f32[6,8,128]{2,1,0:T(8,128)}, f32[1,128]{1,0:T(1,128)}) custom-call(bf16[6,2,1296,128]{3,2,1,0:T(8,128)(2,1)} %bitcast.5, bf16[6,2,1296,128]{3,2,1,0:T(8,128)(2,1)} %bitcast.6), custom_call_target="tpu_custom_call" | custom-call | tf_op jit(solution)/shard_map/pallas_call | solution.py:168
  33.8 1.2 %slice_bitcast_fusion = f32[48]{0:T(128)} fusion(f32[1,128]{1,0:T(1,128)} %get-tuple-element.5), kind=kLoop, calls=%fused_computation | loop fusion | bytes 384 | tf_op jit(solution)/shard_map/squeeze | solution.py:198
  35.0 1.3 %copy.5 = f32[6,2,4,128]{3,2,1,0:T(4,128)} copy(f32[6,2,4,128]{3,2,1,0:T(4,128)} %bitcast.7) | data formatting | bytes 49152
